TPU v7x, 32 devices: a whole 2x2x4 slice. The times are simulated.
32 devices in a mesh: row: 16 (over z, y, core), vec: 2 (over x).
Axes of the slice: x: 2, y: 2, z: 4, core: 2. Of those that a mesh axis runs over, the one named last changes fastest.
Arguments:
- eigvecs: float32 [8192, 2048], P('row', 'vec'), may hold values from -6 to 6
- reflectors: float32 [6, 8192, 128], P(None, 'row', 'vec'), may hold values from -0.375 to 0.375
- factors: float32 [6, 32, 128, 128], P(None, 'row', 'vec'), may hold values from -0.25 to 0.25
Outputs:
- vectors: float32 [8192, 2048], P('row', 'vec')
All inputs are finite; a program needn't handle non-finite values.
Results may differ from a plain program's by a relative error of at most 0.0001.
Values sent between devices are 32-bit elements; how exact they have to be, the bound alone decides.
A program may use at most 64 MiB of HBM per device.

v0:
```python
import functools

import jax
import jax.numpy as jnp
from jax import lax
from jax.experimental import pallas as pl
from jax.experimental.pallas import tpu as pltpu
from jax.sharding import PartitionSpec as P

MESH = pl.DeviceIdType.MESH
CHUNKS = 4


def split(value):
    high = value.astype(jnp.bfloat16)
    return high, (value - high.astype(jnp.float32)).astype(jnp.bfloat16)


def dot(left, right):
    return lax.dot_general(
        left, right, (((1,), (0,)), ((), ())),
        precision=lax.Precision.DEFAULT, preferred_element_type=jnp.float32,
    )


def kernel(
    count, peers, eig, refl, fact, out,
    x, vown, vt, tall, vcat, ucat, wsend, wrecv,
    xin, vin, vsend, vrecv, tsend, trecv, wss, wrs, xout,
):
    rounds, height, share = vown.shape
    nb = vt.shape[1]
    groups = height // (2 * nb)
    chunks, _, wide = x.shape
    d = lax.axis_index("row")
    v = lax.axis_index("vec")

    def peer(o):
        return lax.rem(v + o, peers)

    def rows_of(p):
        return pl.ds(pl.multiple_of(p * share, 8), share)

    def slots(r):
        for k in range(-1 if r % 2 else 0, groups):
            q = k - r // 2
            yield k + 1, q % groups, -(q // groups)

    reach = max(away for r in range(rounds) for _, _, away in slots(r))

    for r in range(rounds):
        pltpu.make_async_copy(refl.at[r], vown.at[r], vin.at[r]).start()
    for c in range(chunks):
        pltpu.make_async_copy(eig.at[:, pl.ds(c * wide, wide)], x.at[c], xin.at[c]).start()

    barrier = pltpu.get_barrier_semaphore()
    valid = jnp.int32(0)
    for away in range(-reach, reach + 1):
        inside = jnp.logical_and(d + away >= 0, d + away < count)
        valid = valid + inside.astype(jnp.int32)

        @pl.when(inside)
        def _():
            for o in range(peers):
                if away != 0 or o != 0:
                    pl.semaphore_signal(
                        barrier, inc=1, device_id=(d + away, peer(o)), device_id_type=MESH
                    )

    pl.semaphore_wait(barrier, valid * peers - 1)

    def t_copy(r, slot, source, away, o):
        return pltpu.make_async_remote_copy(
            src_ref=fact.at[r, source],
            dst_ref=tall.at[r, slot, rows_of(v)],
            send_sem=tsend.at[r, slot, o],
            recv_sem=trecv.at[r, slot],
            device_id=(d + away, peer(o)),
            device_id_type=MESH,
        )

    def v_copy(r, o):
        return pltpu.make_async_remote_copy(
            src_ref=vt.at[r, rows_of(v)],
            dst_ref=vt.at[r, rows_of(v)],
            send_sem=vsend.at[r, o - 1],
            recv_sem=vrecv.at[r, o - 1],
            device_id=(d, peer(o)),
            device_id_type=MESH,
        )

    for r in range(rounds):
        pltpu.make_async_copy(refl.at[r], vown.at[r], vin.at[r]).wait()
        vt[r, rows_of(v)] = jnp.transpose(vown[r])
        for o in range(1, peers):
            v_copy(r, o).start()
        for slot, source, away in slots(r):
            for o in range(peers):
                if away == 0 and o == 0:
                    pltpu.make_async_copy(
                        fact.at[r, source], tall.at[r, slot, rows_of(v)], trecv.at[r, slot]
                    ).start()
                elif away == 0:
                    t_copy(r, slot, source, away, o).start()
                else:
                    @pl.when(d + away < count)
                    def _():
                        t_copy(r, slot, source, away, o).start()

    @pl.when(d == 0)
    def _():
        wrecv[:, 0] = jnp.zeros((rounds // 2, chunks, nb, wide), jnp.float32)

    @pl.when(d == count - 1)
    def _():
        wrecv[:, 1] = jnp.zeros((rounds // 2, chunks, nb, wide), jnp.float32)

    def prepare_v(r):
        for o in range(1, peers):
            part = vt.at[r, rows_of(lax.rem(v + peers - o, peers))]
            pltpu.make_async_copy(part, part, vrecv.at[r, o - 1]).wait()
        vcat[r, :nb], vcat[r, nb:] = split(vt[r])

    def prepare_u(r):
        for slot, _, away in slots(r):
            whole = tall.at[r, slot]
            arrived = pltpu.make_async_copy(whole, whole, trecv.at[r, slot])
            if away == 0:
                arrived.wait()
            else:
                @pl.when(d >= away)
                def _():
                    arrived.wait()

                @pl.when(d < away)
                def _():
                    tall[r, slot] = jnp.zeros((nb, nb), jnp.float32)

            first = (slot - 1) * 2 * nb + (r % 2) * nb
            begin, end = max(first, 0), min(first + 2 * nb, height)
            bh, bl = split(jnp.transpose(vt[r, :, begin:end]))
            th, tl = split(tall[r, slot])
            uh, ul = split(dot(bh, th) + dot(bh, tl) + dot(bl, th))
            ucat[r, begin:end, :nb] = uh
            ucat[r, begin:end, nb : 2 * nb] = ul
            ucat[r, begin:end, 2 * nb :] = uh

    def inner(r, c, begin, end):
        xh, xl = split(x[c, begin:end])
        both = dot(vcat[r, :, begin:end], xh)
        return both[:nb] + both[nb:] + dot(vcat[r, :nb, begin:end], xl)

    def update(r, c, begin, end, w):
        wh, wl = split(w)
        stacked = jnp.concatenate([wh, wh, wl], 0)
        x[c, begin:end] = x[c, begin:end] - dot(ucat[r, begin:end], stacked)

    def even(r, c):
        for g in range(groups):
            begin, end = 2 * nb * g, 2 * nb * (g + 1)
            update(r, c, begin, end, inner(r, c, begin, end))

    def middle(r, c):
        for g in range(groups - 1):
            begin, end = 2 * nb * g + nb, 2 * nb * (g + 1) + nb
            update(r, c, begin, end, inner(r, c, begin, end))

    sides = ((0, nb), (height - nb, height))

    def w_copy(r, c, side):
        return pltpu.make_async_remote_copy(
            src_ref=wsend.at[r // 2, side, c],
            dst_ref=wrecv.at[r // 2, 1 - side, c],
            send_sem=wss.at[r // 2, side, c],
            recv_sem=wrs.at[r // 2, 1 - side, c],
            device_id=(d + 2 * side - 1, v),
            device_id_type=MESH,
        )

    has = (d > 0, d < count - 1)

    def before(r, c):
        for side in (0, 1):
            wsend[r // 2, side, c] = inner(r, c, *sides[side])

            @pl.when(has[side])
            def _():
                w_copy(r, c, side).start()

    def after(r, c):
        for side in (0, 1):
            landed = wrecv.at[r // 2, side, c]

            @pl.when(has[side])
            def _():
                pltpu.make_async_copy(landed, landed, wrs.at[r // 2, side, c]).wait()

            update(r, c, *sides[side], wsend[r // 2, side, c] + wrecv[r // 2, side, c])

    def over_chunks(body):
        lax.fori_loop(0, chunks, lambda c, carry: (body(c), carry)[1], 0)

    prepare_v(0)
    prepare_u(0)
    prepare_v(1)
    for c in range(chunks):
        pltpu.make_async_copy(eig.at[:, pl.ds(c * wide, wide)], x.at[c], xin.at[c]).wait()

    for r in range(1, rounds, 2):
        def step(c):
            if r > 1:
                after(r - 2, c)
            even(r - 1, c)
            before(r, c)

        over_chunks(step)
        prepare_u(r)
        over_chunks(lambda c: middle(r, c))
        if r + 2 < rounds:
            prepare_v(r + 1)
            prepare_u(r + 1)
            prepare_v(r + 2)

    def store(c):
        return pltpu.make_async_copy(
            x.at[c], out.at[:, pl.ds(pl.multiple_of(c * wide, wide), wide)], xout.at[c]
        )

    def finish(c):
        after(rounds - 1, c)
        store(c).start()

    over_chunks(finish)

    for r in range(rounds):
        for o in range(1, peers):
            v_copy(r, o).wait_send()
        for slot, source, away in slots(r):
            for o in range(peers):
                if away == 0 and o != 0:
                    t_copy(r, slot, source, away, o).wait_send()
                elif away != 0:
                    @pl.when(d + away < count)
                    def _():
                        t_copy(r, slot, source, away, o).wait_send()

    for side in (0, 1):
        @pl.when(has[side])
        def _():
            for r in range(1, rounds, 2):
                over_chunks(lambda c: w_copy(r, c, side).wait_send())

    over_chunks(lambda c: store(c).wait())


def solution(mesh):
    count, peers = mesh.shape["row"], mesh.shape["vec"]

    def per_device(eigvecs, reflectors, factors):
        height, width = eigvecs.shape
        rounds, _, share = reflectors.shape
        nb = factors.shape[3]
        groups = height // (2 * nb)
        wide = width // CHUNKS
        f32, bf16, dma = jnp.float32, jnp.bfloat16, pltpu.SemaphoreType.DMA
        links = (rounds // 2, 2, CHUNKS)
        return pl.pallas_call(
            functools.partial(kernel, count, peers),
            out_shape=jax.ShapeDtypeStruct((height, width), f32),
            in_specs=[pl.BlockSpec(memory_space=pl.ANY)] * 3,
            out_specs=pl.BlockSpec(memory_space=pl.ANY),
            scratch_shapes=[
                pltpu.VMEM((CHUNKS, height, wide), f32),
                pltpu.VMEM((rounds, height, share), f32),
                pltpu.VMEM((rounds, nb, height), f32),
                pltpu.VMEM((rounds, groups + 1, nb, nb), f32),
                pltpu.VMEM((rounds, 2 * nb, height), bf16),
                pltpu.VMEM((rounds, height, 3 * nb), bf16),
                pltpu.VMEM(links + (nb, wide), f32),
                pltpu.VMEM(links + (nb, wide), f32),
                dma((CHUNKS,)),
                dma((rounds,)),
                dma((rounds, peers - 1)),
                dma((rounds, peers - 1)),
                dma((rounds, groups + 1, peers)),
                dma((rounds, groups + 1)),
                dma(links),
                dma(links),
                dma((CHUNKS,)),
            ],
            compiler_params=pltpu.CompilerParams(
                collective_id=0, has_side_effects=True, vmem_limit_bytes=48 << 20
            ),
            name="back_transform",
        )(eigvecs, reflectors, factors)

    return jax.shard_map(
        per_device,
        mesh=mesh,
        in_specs=(P("row", "vec"), P(None, "row", "vec"), P(None, "row", "vec", None)),
        out_specs=P("row", "vec"),
        check_vma=False,
    )
```

profile of v0, /device:TPU:25, one launch (start us, length us, event | category | flops | bytes accessed | tf_op | source)
XLA Modules:
  0.0 59.3 jit_solution(8199655467860828054)
XLA Ops:
  0.0 0.0 copy-start.1
  0.0 1.6 %copy.4.refl = f32[6,512,64]{2,1,0:T(8,128)S(1)} copy(f32[6,512,64]{1,2,0:T(8,128)} %param.4) | data formatting | bytes 1572864 | tf_op args[1]
  1.7 0.0 copy-done.1
  1.7 0.0 copy-start
  1.7 1.6 %copy-done = f32[512,1024]{1,0:T(8,128)S(1)} copy-done((f32[512,1024]{1,0:T(8,128)S(1)}, f32[512,1024]{1,0:T(8,128)}, u32[]{:S(2)}) %copy-start) | copy-done | bytes 2097176
  3.3 54.7 %back_transform.1 = f32[512,1024]{1,0:T(8,128)S(1)} custom-call(f32[512,1024]{1,0:T(8,128)S(1)} %copy-done, f32[6,512,64]{2,1,0:T(8,128)S(1)} %copy.4.refl, f32[6,2,64,128]{3,2,1,0:T(8,128)S(1)} %copy-done.1), custom_call_target="tpu_custom_call" | custom-call | tf_op jit(solution)/shard_map/back_transform/pallas_call | solution.py:267
  58.0 1.3 %copy.6 = f32[512,1024]{1,0:T(8,128)} copy(f32[512,1024]{1,0:T(8,128)S(1)} %back_transform.1) | data formatting | bytes 4194304
Async XLA Ops:
  0.0 1.7 %copy-start.1 = (f32[6,2,64,128]{3,2,1,0:T(8,128)S(1)}, f32[6,2,64,128]{3,2,1,0:T(8,128)}, u32[]{:S(2)}) copy-start(f32[6,2,64,128]{3,2,1,0:T(8,128)} %fact.1) | copy-start | bytes 1179652
  1.7 1.6 %copy-start = (f32[512,1024]{1,0:T(8,128)S(1)}, f32[512,1024]{1,0:T(8,128)}, u32[]{:S(2)}) copy-start(f32[512,1024]{1,0:T(8,128)} %eig.1) | copy-start | bytes 6291460
where the time goes:
time: 59.4 us; the launch traced here: 59.3 us
  Pallas kernels  54.7 us (92%)
  local copies, waits for them, and re-layouts  4.56 us (8%)
    pallas_call x1, Pallas kernels, per_device(): pl.pallas_call(functools.partial(kernel, count, peers), out_shape=jax.Sha...  54.7 us
    unnamed x6, local copies, waits for them, and re-layouts  4.56 us

commit v1 on v0

v1 whole, which is shorter than its diff:
```python
import functools

import jax
import jax.numpy as jnp
from jax import lax
from jax.experimental import pallas as pl
from jax.experimental.pallas import tpu as pltpu
from jax.sharding import PartitionSpec as P

MESH = pl.DeviceIdType.MESH
CHUNKS = 4


def split(value):
    high = value.astype(jnp.bfloat16)
    return high, (value - high.astype(jnp.float32)).astype(jnp.bfloat16)


def dot(left, right):
    return lax.dot_general(
        left, right, (((1,), (0,)), ((), ())),
        precision=lax.Precision.DEFAULT, preferred_element_type=jnp.float32,
    )


def kernel(
    count, peers, eig, refl, fact, out,
    x, vt, tall, vcat, ucat, wsend, wrecv,
    xin, vsend, vrecv, tsend, trecv, wss, wrs, xout,
):
    rounds, nb, height = vt.shape
    share = refl.shape[1]
    groups = height // (2 * nb)
    chunks, _, wide = x.shape
    d = lax.axis_index("row")
    v = lax.axis_index("vec")
    odd = lax.rem(d, 2)

    def peer(o):
        return lax.rem(v + o, peers)

    def rows_of(p):
        return pl.ds(pl.multiple_of(p * share, 8), share)

    def turn(i, last):
        return i + odd * (last - 2 * i)

    def group_rows(i):
        return pl.ds(pl.multiple_of(turn(i, groups - 1) * 2 * nb, nb), 2 * nb)

    def side_rows(i):
        return pl.ds(pl.multiple_of(turn(i, 1) * (height - nb), nb), nb)

    def middle_rows(g):
        return pl.ds(2 * nb * g + nb, 2 * nb)

    def pieces(r):
        if r == 0:
            return [group_rows(i) for i in range(groups)]
        if r == 1:
            return [side_rows(0), side_rows(1)] + [pl.ds(nb, height - 2 * nb)]
        return [pl.ds(0, height)]

    def slots(r):
        for k in range(-1 if r % 2 else 0, groups):
            q = k - r // 2
            yield k + 1, q % groups, -(q // groups)

    reach = max(away for r in range(rounds) for _, _, away in slots(r))

    def load(c):
        return pltpu.make_async_copy(eig.at[:, pl.ds(c * wide, wide)], x.at[c], xin.at[c])

    barrier = pltpu.get_barrier_semaphore()
    valid = jnp.int32(0)
    for away in range(-reach, reach + 1):
        inside = jnp.logical_and(d + away >= 0, d + away < count)
        valid = valid + inside.astype(jnp.int32)

        @pl.when(inside)
        def _():
            for o in range(peers):
                if away != 0 or o != 0:
                    pl.semaphore_signal(
                        barrier, inc=1, device_id=(d + away, peer(o)), device_id_type=MESH
                    )

    for c in range(chunks):
        load(c).start()
    pl.semaphore_wait(barrier, valid * peers - 1)

    def t_copy(r, slot, source, away, o):
        return pltpu.make_async_remote_copy(
            src_ref=fact.at[r, source],
            dst_ref=tall.at[r, slot, rows_of(v)],
            send_sem=tsend.at[r, slot, o],
            recv_sem=trecv.at[r, slot],
            device_id=(d + away, peer(o)),
            device_id_type=MESH,
        )

    def v_copy(r, piece, where, o):
        return pltpu.make_async_remote_copy(
            src_ref=refl.at[r, :, where],
            dst_ref=vt.at[r, rows_of(v), where],
            send_sem=vsend.at[r, piece, o],
            recv_sem=vrecv.at[r, piece, o],
            device_id=(d, peer(o)),
            device_id_type=MESH,
        )

    def send_v(r, piece):
        where = pieces(r)[piece]
        for o in range(1, peers):
            v_copy(r, piece, where, o).start()
        pltpu.make_async_copy(
            refl.at[r, :, where], vt.at[r, rows_of(v), where], vrecv.at[r, piece, 0]
        ).start()

    def send_t(r, slot, source, away):
        for o in range(peers):
            if not isinstance(away, int) or away != 0:
                @pl.when(d + away < count)
                def _():
                    t_copy(r, slot, source, away, o).start()
            elif o != 0:
                t_copy(r, slot, source, away, o).start()
            else:
                pltpu.make_async_copy(
                    fact.at[r, source], tall.at[r, slot, rows_of(v)], trecv.at[r, slot]
                ).start()

    def send_round(r):
        for piece in range(len(pieces(r))):
            send_v(r, piece)
        for entry in slots(r):
            send_t(r, *entry)

    for i in range(groups):
        g = turn(i, groups - 1)
        send_v(0, i)
        send_t(0, g + 1, g, 0)
        if i == 0:
            send_v(1, 0)
    send_v(1, 1)
    send_v(1, 2)
    for entry in slots(1):
        send_t(1, *entry)

    @pl.when(d == 0)
    def _():
        wrecv[:, 0] = jnp.zeros((rounds // 2, chunks, nb, wide), jnp.float32)

    @pl.when(d == count - 1)
    def _():
        wrecv[:, 1] = jnp.zeros((rounds // 2, chunks, nb, wide), jnp.float32)

    def prepare_v(r, piece):
        where = pieces(r)[piece]
        for o in range(peers):
            part = vt.at[r, rows_of(lax.rem(v + peers - o, peers)), where]
            pltpu.make_async_copy(part, part, vrecv.at[r, piece, o]).wait()
        high, low = split(vt[r, :, where])
        vcat[r, :nb, where] = high
        vcat[r, nb:, where] = low

    def form_u(r, slot, where):
        bh, bl = split(jnp.transpose(vt[r, :, where]))
        th, tl = split(tall[r, slot])
        uh, ul = split(dot(bh, th) + dot(bh, tl) + dot(bl, th))
        ucat[r, where, :nb] = uh
        ucat[r, where, nb : 2 * nb] = ul
        ucat[r, where, 2 * nb :] = uh

    def arrived(r, slot):
        whole = tall.at[r, slot]
        return pltpu.make_async_copy(whole, whole, trecv.at[r, slot])

    def prepare_u(r):
        for slot, _, away in slots(r):
            if away == 0:
                arrived(r, slot).wait()
            else:
                @pl.when(d >= away)
                def _():
                    arrived(r, slot).wait()

                @pl.when(d < away)
                def _():
                    tall[r, slot] = jnp.zeros((nb, nb), jnp.float32)

            first = (slot - 1) * 2 * nb + (r % 2) * nb
            begin, end = max(first, 0), min(first + 2 * nb, height)
            form_u(r, slot, pl.ds(begin, end - begin))

    def inner(r, c, rows):
        xh, xl = split(x[c, rows])
        both = dot(vcat[r, :, rows], xh)
        return both[:nb] + both[nb:] + dot(vcat[r, :nb, rows], xl)

    def update(r, c, rows, w):
        wh, wl = split(w)
        stacked = jnp.concatenate([wh, wh, wl], 0)
        x[c, rows] = x[c, rows] - dot(ucat[r, rows], stacked)

    def apply(r, c, rows):
        update(r, c, rows, inner(r, c, rows))

    def middle(r, c):
        for g in range(groups - 1):
            apply(r, c, middle_rows(g))

    def neighbour(i):
        return d + 2 * turn(i, 1) - 1

    def reachable(i):
        return jnp.logical_and(neighbour(i) >= 0, neighbour(i) < count)

    def w_copy(r, c, i):
        side = turn(i, 1)
        return pltpu.make_async_remote_copy(
            src_ref=wsend.at[r // 2, side, c],
            dst_ref=wrecv.at[r // 2, 1 - side, c],
            send_sem=wss.at[r // 2, side, c],
            recv_sem=wrs.at[r // 2, 1 - side, c],
            device_id=(neighbour(i), v),
            device_id_type=MESH,
        )

    def before(r, c, i):
        wsend[r // 2, turn(i, 1), c] = inner(r, c, side_rows(i))

        @pl.when(reachable(i))
        def _():
            w_copy(r, c, i).start()

    def after(r, c, i):
        side = turn(i, 1)
        landed = wrecv.at[r // 2, side, c]

        @pl.when(reachable(i))
        def _():
            pltpu.make_async_copy(landed, landed, wrs.at[r // 2, side, c]).wait()

        update(r, c, side_rows(i), wsend[r // 2, side, c] + wrecv[r // 2, side, c])

    def over_chunks(body):
        lax.fori_loop(0, chunks, lambda c, carry: (body(c), carry)[1], 0)

    for i in range(groups):
        g = turn(i, groups - 1)
        prepare_v(0, i)
        if i == 0:
            for r in range(2, rounds, 2):
                send_round(r)
                send_round(r + 1)
        arrived(0, g + 1).wait()
        form_u(0, g + 1, group_rows(i))
        if i == 0:
            for c in range(chunks):
                load(c).wait()
        over_chunks(lambda c: apply(0, c, group_rows(i)))
        if i == 0:
            prepare_v(1, 0)
            over_chunks(lambda c: before(1, c, 0))
    prepare_v(1, 1)
    over_chunks(lambda c: before(1, c, 1))
    prepare_v(1, 2)
    prepare_u(1)
    over_chunks(lambda c: middle(1, c))

    for r in range(2, rounds, 2):
        prepare_v(r, 0)
        prepare_u(r)
        prepare_v(r + 1, 0)

        def step(c):
            for i in range(groups):
                if i < 2:
                    after(r - 1, c, i)
                apply(r, c, group_rows(i))
                if i == 0:
                    before(r + 1, c, 0)
            before(r + 1, c, 1)

        over_chunks(step)
        prepare_u(r + 1)
        over_chunks(lambda c: middle(r + 1, c))

    def store(c):
        return pltpu.make_async_copy(
            x.at[c], out.at[:, pl.ds(pl.multiple_of(c * wide, wide), wide)], xout.at[c]
        )

    def finish(c):
        after(rounds - 1, c, 0)
        after(rounds - 1, c, 1)
        store(c).start()

    over_chunks(finish)

    for r in range(rounds):
        for piece, where in enumerate(pieces(r)):
            for o in range(1, peers):
                v_copy(r, piece, where, o).wait_send()
        for slot, source, away in slots(r):
            for o in range(peers):
                if away == 0 and o != 0:
                    t_copy(r, slot, source, away, o).wait_send()
                elif away != 0:
                    @pl.when(d + away < count)
                    def _():
                        t_copy(r, slot, source, away, o).wait_send()

    for i in (0, 1):
        @pl.when(reachable(i))
        def _():
            for r in range(1, rounds, 2):
                over_chunks(lambda c: w_copy(r, c, i).wait_send())

    over_chunks(lambda c: store(c).wait())


def solution(mesh):
    count, peers = mesh.shape["row"], mesh.shape["vec"]

    def per_device(eigvecs, reflectors, factors):
        height, width = eigvecs.shape
        rounds = reflectors.shape[0]
        nb = factors.shape[3]
        groups = height // (2 * nb)
        wide = width // CHUNKS
        f32, bf16, dma = jnp.float32, jnp.bfloat16, pltpu.SemaphoreType.DMA
        links = (rounds // 2, 2, CHUNKS)
        return pl.pallas_call(
            functools.partial(kernel, count, peers),
            out_shape=jax.ShapeDtypeStruct((height, width), f32),
            in_specs=[pl.BlockSpec(memory_space=pltpu.HBM)] * 3,
            out_specs=pl.BlockSpec(memory_space=pl.ANY),
            scratch_shapes=[
                pltpu.VMEM((CHUNKS, height, wide), f32),
                pltpu.VMEM((rounds, nb, height), f32),
                pltpu.VMEM((rounds, groups + 1, nb, nb), f32),
                pltpu.VMEM((rounds, 2 * nb, height), bf16),
                pltpu.VMEM((rounds, height, 3 * nb), bf16),
                pltpu.VMEM(links + (nb, wide), f32),
                pltpu.VMEM(links + (nb, wide), f32),
                dma((CHUNKS,)),
                dma((rounds, 3, peers)),
                dma((rounds, 3, peers)),
                dma((rounds, groups + 1, peers)),
                dma((rounds, groups + 1)),
                dma(links),
                dma(links),
                dma((CHUNKS,)),
            ],
            compiler_params=pltpu.CompilerParams(
                collective_id=0, has_side_effects=True, vmem_limit_bytes=64500000
            ),
            name="back_transform",
        )(eigvecs, jnp.transpose(reflectors, (0, 2, 1)), factors)

    return jax.shard_map(
        per_device,
        mesh=mesh,
        in_specs=(P("row", "vec"), P(None, "row", "vec"), P(None, "row", "vec", None)),
        out_specs=P("row", "vec"),
        check_vma=False,
    )
```

time: 59.4 us -> 56 us (0.943); the launches traced: 59.3 us -> 55 us
  Pallas kernels: 54.7 us -> 51.8 us
  local copies, waits for them, and re-layouts: 4.56 us -> 3.16 us
    pallas_call x1, Pallas kernels: 54.7 us -> 51.8 us  [per_device(): pl.pallas_call(functools.partial(kernel, count, peers), out_shape=jax.Sha...]
    unnamed x6 -> x1, local copies, waits for them, and re-layouts: 4.56 us -> 3.16 us
where the time goes in v1:
time: 56 us; the launch traced here: 55 us
  Pallas kernels  51.8 us (92%)
  local copies, waits for them, and re-layouts  3.16 us (6%)
    pallas_call x1, Pallas kernels, per_device(): pl.pallas_call(functools.partial(kernel, count, peers), out_shape=jax.Sha...  51.8 us
    unnamed x1, local copies, waits for them, and re-layouts  3.16 us

profile of v1, /device:TPU:25, one launch (start us, length us, event | category | flops | bytes accessed | tf_op | source)
XLA Modules:
  0.0 55.0 jit_solution(1898983648199724487)
XLA Ops:
  0.0 51.8 %back_transform.1 = f32[512,1024]{1,0:T(8,128)} custom-call(f32[512,1024]{1,0:T(8,128)} %eig.1, f32[6,64,512]{2,1,0:T(8,128)} %bitcast.1, f32[6,2,64,128]{3,2,1,0:T(8,128)} %fact.1), custom_call_target="tpu_custom_call" | custom-call | tf_op jit(solution)/shard_map/back_transform/pallas_call | solution.py:335
  51.8 3.2 %copy.5 = f32[512,1024]{1,0:T(8,128)} copy(f32[512,1024]{1,0:T(8,128)} %back_transform.1) | data formatting | bytes 4194304

commit v2 on v1

--- a/solution.py
+++ b/solution.py
@@ -90,12 +90,13 @@
     pl.semaphore_wait(barrier, valid * peers - 1)
 
     def t_copy(r, slot, source, away, o):
+        mine = tall.at[r, slot, rows_of(v)]
         return pltpu.make_async_remote_copy(
-            src_ref=fact.at[r, source],
-            dst_ref=tall.at[r, slot, rows_of(v)],
+            src_ref=fact.at[r, source] if o == 0 or away == 0 else mine,
+            dst_ref=mine,
             send_sem=tsend.at[r, slot, o],
-            recv_sem=trecv.at[r, slot],
-            device_id=(d + away, peer(o)),
+            recv_sem=trecv.at[r, slot, o],
+            device_id=(d + away if o == 0 else d, peer(o)),
             device_id_type=MESH,
         )
 
@@ -117,18 +118,26 @@
             refl.at[r, :, where], vt.at[r, rows_of(v), where], vrecv.at[r, piece, 0]
         ).start()
 
+    def own_t(r, slot, source):
+        return pltpu.make_async_copy(
+            fact.at[r, source], tall.at[r, slot, rows_of(v)], trecv.at[r, slot, 0]
+        )
+
+    def landed_t(r, slot, o):
+        part = tall.at[r, slot, rows_of(lax.rem(v + peers - o, peers))]
+        return pltpu.make_async_copy(part, part, trecv.at[r, slot, o])
+
     def send_t(r, slot, source, away):
-        for o in range(peers):
-            if not isinstance(away, int) or away != 0:
-                @pl.when(d + away < count)
-                def _():
+        if away == 0:
+            own_t(r, slot, source).start()
+            for o in range(1, peers):
+                t_copy(r, slot, source, away, o).start()
+        else:
+            @pl.when(d >= away)
+            def _():
+                landed_t(r, slot, 0).wait()
+                for o in range(1, peers):
                     t_copy(r, slot, source, away, o).start()
-            elif o != 0:
-                t_copy(r, slot, source, away, o).start()
-            else:
-                pltpu.make_async_copy(
-                    fact.at[r, source], tall.at[r, slot, rows_of(v)], trecv.at[r, slot]
-                ).start()
 
     def send_round(r):
         for piece in range(len(pieces(r))):
@@ -136,16 +145,22 @@
         for entry in slots(r):
             send_t(r, *entry)
 
+    send_v(0, 0)
+    for r in range(rounds):
+        for slot, source, away in slots(r):
+            if away != 0:
+                @pl.when(d + away < count)
+                def _():
+                    t_copy(r, slot, source, away, 0).start()
     for i in range(groups):
         g = turn(i, groups - 1)
-        send_v(0, i)
+        if i > 0:
+            send_v(0, i)
         send_t(0, g + 1, g, 0)
         if i == 0:
             send_v(1, 0)
     send_v(1, 1)
     send_v(1, 2)
-    for entry in slots(1):
-        send_t(1, *entry)
 
     @pl.when(d == 0)
     def _():
@@ -172,18 +187,18 @@
         ucat[r, where, nb : 2 * nb] = ul
         ucat[r, where, 2 * nb :] = uh
 
-    def arrived(r, slot):
-        whole = tall.at[r, slot]
-        return pltpu.make_async_copy(whole, whole, trecv.at[r, slot])
+    def arrived(r, slot, away):
+        for o in range(0 if away == 0 else 1, peers):
+            landed_t(r, slot, o).wait()
 
     def prepare_u(r):
         for slot, _, away in slots(r):
             if away == 0:
-                arrived(r, slot).wait()
+                arrived(r, slot, away)
             else:
                 @pl.when(d >= away)
                 def _():
-                    arrived(r, slot).wait()
+                    arrived(r, slot, away)
 
                 @pl.when(d < away)
                 def _():
@@ -193,18 +208,19 @@
             begin, end = max(first, 0), min(first + 2 * nb, height)
             form_u(r, slot, pl.ds(begin, end - begin))
 
-    def inner(r, c, rows):
-        xh, xl = split(x[c, rows])
+    def inner(r, rows, value):
+        xh, xl = split(value)
         both = dot(vcat[r, :, rows], xh)
         return both[:nb] + both[nb:] + dot(vcat[r, :nb, rows], xl)
 
-    def update(r, c, rows, w):
+    def updated(r, rows, value, w):
         wh, wl = split(w)
         stacked = jnp.concatenate([wh, wh, wl], 0)
-        x[c, rows] = x[c, rows] - dot(ucat[r, rows], stacked)
+        return value - dot(ucat[r, rows], stacked)
 
     def apply(r, c, rows):
-        update(r, c, rows, inner(r, c, rows))
+        value = x[c, rows]
+        x[c, rows] = updated(r, rows, value, inner(r, rows, value))
 
     def middle(r, c):
         for g in range(groups - 1):
@@ -228,21 +244,25 @@
         )
 
     def before(r, c, i):
-        wsend[r // 2, turn(i, 1), c] = inner(r, c, side_rows(i))
+        wsend[r // 2, turn(i, 1), c] = inner(r, side_rows(i), x[c, side_rows(i)])
 
         @pl.when(reachable(i))
         def _():
             w_copy(r, c, i).start()
 
-    def after(r, c, i):
-        side = turn(i, 1)
-        landed = wrecv.at[r // 2, side, c]
-
-        @pl.when(reachable(i))
-        def _():
-            pltpu.make_async_copy(landed, landed, wrs.at[r // 2, side, c]).wait()
-
-        update(r, c, side_rows(i), wsend[r // 2, side, c] + wrecv[r // 2, side, c])
+    ends = (slice(0, nb), slice(height - nb, height))
+
+    def after(r, c):
+        for i in (0, 1):
+            @pl.when(reachable(i))
+            def _():
+                landed = wrecv.at[r // 2, turn(i, 1), c]
+                pltpu.make_async_copy(landed, landed, wrs.at[r // 2, turn(i, 1), c]).wait()
+
+        return [
+            updated(r, rows, x[c, rows], wsend[r // 2, side, c] + wrecv[r // 2, side, c])
+            for side, rows in enumerate(ends)
+        ]
 
     def over_chunks(body):
         lax.fori_loop(0, chunks, lambda c, carry: (body(c), carry)[1], 0)
@@ -251,10 +271,11 @@
         g = turn(i, groups - 1)
         prepare_v(0, i)
         if i == 0:
-            for r in range(2, rounds, 2):
-                send_round(r)
-                send_round(r + 1)
-        arrived(0, g + 1).wait()
+            for entry in slots(1):
+                send_t(1, *entry)
+            send_round(2)
+            send_round(3)
+        arrived(0, g + 1, 0)
         form_u(0, g + 1, group_rows(i))
         if i == 0:
             for c in range(chunks):
@@ -263,11 +284,14 @@
         if i == 0:
             prepare_v(1, 0)
             over_chunks(lambda c: before(1, c, 0))
+            for r in range(4, rounds):
+                send_round(r)
     prepare_v(1, 1)
     over_chunks(lambda c: before(1, c, 1))
     prepare_v(1, 2)
     prepare_u(1)
-    over_chunks(lambda c: middle(1, c))
+    for c in range(chunks):
+        middle(1, c)
 
     for r in range(2, rounds, 2):
         prepare_v(r, 0)
@@ -275,17 +299,27 @@
         prepare_v(r + 1, 0)
 
         def step(c):
-            for i in range(groups):
-                if i < 2:
-                    after(r - 1, c, i)
-                apply(r, c, group_rows(i))
-                if i == 0:
-                    before(r + 1, c, 0)
-            before(r + 1, c, 1)
+            head, tail = after(r - 1, c)
+            whole = jnp.concatenate([head, x[c, nb : height - nb], tail], 0)
+            spans = [slice(2 * nb * g, 2 * nb * (g + 1)) for g in range(groups)]
+            shares = [inner(r, rows, whole[rows]) for rows in spans]
+            values = [updated(r, rows, whole[rows], w) for rows, w in zip(spans, shares)]
+            strips = (values[0][:nb], values[-1][nb:])
+            shares = [inner(r + 1, rows, strip) for rows, strip in zip(ends, strips)]
+            for side in (0, 1):
+                wsend[(r + 1) // 2, side, c] = shares[side]
+            for i in (0, 1):
+                @pl.when(reachable(i))
+                def _():
+                    w_copy(r + 1, c, i).start()
+
+            for rows, value in zip(spans, values):
+                x[c, rows] = value
 
         over_chunks(step)
         prepare_u(r + 1)
-        over_chunks(lambda c: middle(r + 1, c))
+        for c in range(chunks):
+            middle(r + 1, c)
 
     def store(c):
         return pltpu.make_async_copy(
@@ -293,8 +327,8 @@
         )
 
     def finish(c):
-        after(rounds - 1, c, 0)
-        after(rounds - 1, c, 1)
+        for rows, value in zip(ends, after(rounds - 1, c)):
+            x[c, rows] = value
         store(c).start()
 
     over_chunks(finish)
@@ -308,7 +342,7 @@
                 if away == 0 and o != 0:
                     t_copy(r, slot, source, away, o).wait_send()
                 elif away != 0:
-                    @pl.when(d + away < count)
+                    @pl.when(d + away < count if o == 0 else d >= away)
                     def _():
                         t_copy(r, slot, source, away, o).wait_send()
 
@@ -349,16 +383,21 @@
                 dma((rounds, 3, peers)),
                 dma((rounds, 3, peers)),
                 dma((rounds, groups + 1, peers)),
-                dma((rounds, groups + 1)),
+                dma((rounds, groups + 1, peers)),
                 dma(links),
                 dma(links),
                 dma((CHUNKS,)),
             ],
             compiler_params=pltpu.CompilerParams(
-                collective_id=0, has_side_effects=True, vmem_limit_bytes=64500000
+                collective_id=0, has_side_effects=True, vmem_limit_bytes=48 << 20
             ),
             name="back_transform",
-        )(eigvecs, jnp.transpose(reflectors, (0, 2, 1)), factors)
+        )(
+            *(
+                pltpu.with_memory_space_constraint(array, pltpu.HBM)
+                for array in (eigvecs, jnp.transpose(reflectors, (0, 2, 1)), factors)
+            )
+        )
 
     return jax.shard_map(
         per_device,

time: 56 us -> 49.4 us (0.88); the launches traced: 55 us -> 49.3 us
  Pallas kernels: 51.8 us -> 47.9 us
  local copies, waits for them, and re-layouts: 3.16 us -> 1.32 us
    pallas_call x1, Pallas kernels: 51.8 us -> 47.9 us  [per_device(): pl.pallas_call(functools.partial(kernel, count, peers), out_shape=jax.Sha...]
    unnamed x1, local copies, waits for them, and re-layouts: 3.16 us -> 1.32 us
where the time goes in v2:
time: 49.4 us; the launch traced here: 49.3 us
  Pallas kernels  47.9 us (97%)
  local copies, waits for them, and re-layouts  1.32 us (3%)
    pallas_call x1, Pallas kernels, per_device(): pl.pallas_call(functools.partial(kernel, count, peers), out_shape=jax.Sha...  47.9 us
    unnamed x1, local copies, waits for them, and re-layouts  1.32 us

profile of v2, /device:TPU:25, one launch (start us, length us, event | category | flops | bytes accessed | tf_op | source)
XLA Modules:
  0.0 49.3 jit_solution(12441617193014608874)
XLA Ops:
  0.0 47.9 %back_transform.1 = f32[512,1024]{1,0:T(8,128)S(1)} custom-call(f32[512,1024]{1,0:T(8,128)} %eig.1, f32[6,64,512]{2,1,0:T(8,128)} %bitcast.1, f32[6,2,64,128]{3,2,1,0:T(8,128)} %fact.1), custom_call_target="tpu_custom_call" | custom-call | tf_op jit(solution)/shard_map/back_transform/pallas_call | solution.py:369
  48.0 1.3 %copy.5 = f32[512,1024]{1,0:T(8,128)} copy(f32[512,1024]{1,0:T(8,128)S(1)} %back_transform.1) | data formatting | bytes 4194304

commit v3 on v2

--- a/solution.py
+++ b/solution.py
@@ -26,7 +26,7 @@
 def kernel(
     count, peers, eig, refl, fact, out,
     x, vt, tall, vcat, ucat, wsend, wrecv,
-    xin, vsend, vrecv, tsend, trecv, wss, wrs, xout,
+    xin, vsend, vrecv, tsend, trecv, hsend, hrecv, wss, wrs, xout,
 ):
     rounds, nb, height = vt.shape
     share = refl.shape[1]
@@ -57,7 +57,7 @@
     def pieces(r):
         if r == 0:
             return [group_rows(i) for i in range(groups)]
-        if r == 1:
+        if r % 2 == 1:
             return [side_rows(0), side_rows(1)] + [pl.ds(nb, height - 2 * nb)]
         return [pl.ds(0, height)]
 
@@ -65,6 +65,25 @@
         for k in range(-1 if r % 2 else 0, groups):
             q = k - r // 2
             yield k + 1, q % groups, -(q // groups)
+
+    def sends_row(slot, away):
+        there = d + away < count
+        return jnp.logical_and(there, lax.rem(d + away, 2) == 0) if slot == 0 else there
+
+    def takes_row(slot, away):
+        return jnp.logical_and(d >= away, odd == 0) if slot == 0 else d >= away
+
+    def head_copy(r):
+        return pltpu.make_async_remote_copy(
+            src_ref=tall.at[r, groups],
+            dst_ref=tall.at[r, 0],
+            send_sem=hsend.at[r],
+            recv_sem=hrecv.at[r],
+            device_id=(d + 1, v),
+            device_id_type=MESH,
+        )
+
+    gives_head = jnp.logical_and(odd == 0, d + 1 < count)
 
     reach = max(away for r in range(rounds) for _, _, away in slots(r))
 
@@ -133,7 +152,7 @@
             for o in range(1, peers):
                 t_copy(r, slot, source, away, o).start()
         else:
-            @pl.when(d >= away)
+            @pl.when(takes_row(slot, away))
             def _():
                 landed_t(r, slot, 0).wait()
                 for o in range(1, peers):
@@ -149,7 +168,7 @@
     for r in range(rounds):
         for slot, source, away in slots(r):
             if away != 0:
-                @pl.when(d + away < count)
+                @pl.when(sends_row(slot, away))
                 def _():
                     t_copy(r, slot, source, away, 0).start()
     for i in range(groups):
@@ -192,17 +211,27 @@
             landed_t(r, slot, o).wait()
 
     def prepare_u(r):
-        for slot, _, away in slots(r):
+        for slot, _, away in reversed(list(slots(r))):
             if away == 0:
                 arrived(r, slot, away)
             else:
-                @pl.when(d >= away)
+                @pl.when(takes_row(slot, away))
                 def _():
                     arrived(r, slot, away)
 
-                @pl.when(d < away)
+                @pl.when(d < away if slot else jnp.logical_and(d < away, odd == 0))
                 def _():
                     tall[r, slot] = jnp.zeros((nb, nb), jnp.float32)
+
+            if r % 2 == 1 and slot == groups:
+                @pl.when(gives_head)
+                def _():
+                    head_copy(r).start()
+
+            if slot == 0:
+                @pl.when(odd == 1)
+                def _():
+                    head_copy(r).wait_recv()
 
             first = (slot - 1) * 2 * nb + (r % 2) * nb
             begin, end = max(first, 0), min(first + 2 * nb, height)
@@ -243,12 +272,19 @@
             device_id_type=MESH,
         )
 
-    def before(r, c, i):
-        wsend[r // 2, turn(i, 1), c] = inner(r, side_rows(i), x[c, side_rows(i)])
-
-        @pl.when(reachable(i))
-        def _():
-            w_copy(r, c, i).start()
+    def first(c, i, side):
+        rows = group_rows(i)
+        value = x[c, rows]
+        value = updated(0, rows, value, inner(0, rows, value))
+        if side is not None:
+            strip = jnp.where(odd == side, value[:nb], value[nb:])
+            wsend[0, turn(side, 1), c] = inner(1, side_rows(side), strip)
+
+            @pl.when(reachable(side))
+            def _():
+                w_copy(1, c, side).start()
+
+        x[c, rows] = value
 
     ends = (slice(0, nb), slice(height - nb, height))
 
@@ -280,14 +316,13 @@
         if i == 0:
             for c in range(chunks):
                 load(c).wait()
-        over_chunks(lambda c: apply(0, c, group_rows(i)))
+        side = {0: 0, groups - 1: 1}.get(i)
+        if side is not None:
+            prepare_v(1, side)
+        over_chunks(lambda c: first(c, i, side))
         if i == 0:
-            prepare_v(1, 0)
-            over_chunks(lambda c: before(1, c, 0))
             for r in range(4, rounds):
                 send_round(r)
-    prepare_v(1, 1)
-    over_chunks(lambda c: before(1, c, 1))
     prepare_v(1, 2)
     prepare_u(1)
     for c in range(chunks):
@@ -297,6 +332,7 @@
         prepare_v(r, 0)
         prepare_u(r)
         prepare_v(r + 1, 0)
+        prepare_v(r + 1, 1)
 
         def step(c):
             head, tail = after(r - 1, c)
@@ -317,6 +353,7 @@
                 x[c, rows] = value
 
         over_chunks(step)
+        prepare_v(r + 1, 2)
         prepare_u(r + 1)
         for c in range(chunks):
             middle(r + 1, c)
@@ -342,7 +379,7 @@
                 if away == 0 and o != 0:
                     t_copy(r, slot, source, away, o).wait_send()
                 elif away != 0:
-                    @pl.when(d + away < count if o == 0 else d >= away)
+                    @pl.when(sends_row(slot, away) if o == 0 else takes_row(slot, away))
                     def _():
                         t_copy(r, slot, source, away, o).wait_send()
 
@@ -351,6 +388,11 @@
         def _():
             for r in range(1, rounds, 2):
                 over_chunks(lambda c: w_copy(r, c, i).wait_send())
+
+    @pl.when(gives_head)
+    def _():
+        for r in range(1, rounds, 2):
+            head_copy(r).wait_send()
 
     over_chunks(lambda c: store(c).wait())
 
@@ -384,6 +426,8 @@
                 dma((rounds, 3, peers)),
                 dma((rounds, groups + 1, peers)),
                 dma((rounds, groups + 1, peers)),
+                dma((rounds,)),
+                dma((rounds,)),
                 dma(links),
                 dma(links),
                 dma((CHUNKS,)),

time: 49.4 us -> 47.5 us (0.962)
  Pallas kernels: 47.9 us -> 46 us
    pallas_call x1, Pallas kernels: 47.9 us -> 46 us  [per_device(): pl.pallas_call(functools.partial(kernel, count, peers), out_shape=jax.Sha...]
where the time goes in v3:
time: 47.5 us; the launch traced here: 47.3 us
  Pallas kernels  46 us (97%)
  local copies, waits for them, and re-layouts  1.32 us (3%)
    pallas_call x1, Pallas kernels, per_device(): pl.pallas_call(functools.partial(kernel, count, peers), out_shape=jax.Sha...  46 us
    unnamed x1, local copies, waits for them, and re-layouts  1.32 us

profile of v3, /device:TPU:25, one launch (start us, length us, event | category | flops | bytes accessed | tf_op | source)
XLA Modules:
  0.0 47.3 jit_solution(4691183708050812813)
XLA Ops:
  0.0 46.0 %back_transform.1 = f32[512,1024]{1,0:T(8,128)S(1)} custom-call(f32[512,1024]{1,0:T(8,128)} %eig.1, f32[6,64,512]{2,1,0:T(8,128)} %bitcast.1, f32[6,2,64,128]{3,2,1,0:T(8,128)} %fact.1), custom_call_target="tpu_custom_call" | custom-call | tf_op jit(solution)/shard_map/back_transform/pallas_call | solution.py:411
  46.0 1.3 %copy.5 = f32[512,1024]{1,0:T(8,128)} copy(f32[512,1024]{1,0:T(8,128)S(1)} %back_transform.1) | data formatting | bytes 4194304

commit v4 on v3

--- a/solution.py
+++ b/solution.py
@@ -94,19 +94,19 @@
     valid = jnp.int32(0)
     for away in range(-reach, reach + 1):
         inside = jnp.logical_and(d + away >= 0, d + away < count)
-        valid = valid + inside.astype(jnp.int32)
+        partners = [o for o in range(peers) if (away == 0) != (o == 0)]
+        valid = valid + inside.astype(jnp.int32) * len(partners)
 
         @pl.when(inside)
         def _():
-            for o in range(peers):
-                if away != 0 or o != 0:
-                    pl.semaphore_signal(
-                        barrier, inc=1, device_id=(d + away, peer(o)), device_id_type=MESH
-                    )
+            for o in partners:
+                pl.semaphore_signal(
+                    barrier, inc=1, device_id=(d + away, peer(o)), device_id_type=MESH
+                )
 
     for c in range(chunks):
         load(c).start()
-    pl.semaphore_wait(barrier, valid * peers - 1)
+    pl.semaphore_wait(barrier, valid)
 
     def t_copy(r, slot, source, away, o):
         mine = tall.at[r, slot, rows_of(v)]
@@ -306,11 +306,6 @@
     for i in range(groups):
         g = turn(i, groups - 1)
         prepare_v(0, i)
-        if i == 0:
-            for entry in slots(1):
-                send_t(1, *entry)
-            send_round(2)
-            send_round(3)
         arrived(0, g + 1, 0)
         form_u(0, g + 1, group_rows(i))
         if i == 0:
@@ -321,6 +316,11 @@
             prepare_v(1, side)
         over_chunks(lambda c: first(c, i, side))
         if i == 0:
+            for entry in slots(1):
+                send_t(1, *entry)
+            send_round(2)
+            send_round(3)
+        if i == groups - 1:
             for r in range(4, rounds):
                 send_round(r)
     prepare_v(1, 2)

time: 47.5 us -> 47.4 us (level)
  no operation moved by 1% of the time
where the time goes in v4:
time: 47.4 us; the launch traced here: 47.2 us
  Pallas kernels  45.9 us (97%)
  local copies, waits for them, and re-layouts  1.32 us (3%)
    pallas_call x1, Pallas kernels, per_device(): pl.pallas_call(functools.partial(kernel, count, peers), out_shape=jax.Sha...  45.9 us
    unnamed x1, local copies, waits for them, and re-layouts  1.32 us

profile of v4, /device:TPU:25, one launch (start us, length us, event | category | flops | bytes accessed | tf_op | source)
XLA Modules:
  0.0 47.2 jit_solution(1702750564006070750)
XLA Ops:
  0.0 45.9 %back_transform.1 = f32[512,1024]{1,0:T(8,128)S(1)} custom-call(f32[512,1024]{1,0:T(8,128)} %eig.1, f32[6,64,512]{2,1,0:T(8,128)} %bitcast.1, f32[6,2,64,128]{3,2,1,0:T(8,128)} %fact.1), custom_call_target="tpu_custom_call" | custom-call | tf_op jit(solution)/shard_map/back_transform/pallas_call | solution.py:411
  45.9 1.3 %copy.5 = f32[512,1024]{1,0:T(8,128)} copy(f32[512,1024]{1,0:T(8,128)S(1)} %back_transform.1) | data formatting | bytes 4194304

commit v5 on v4

--- a/solution.py
+++ b/solution.py
@@ -306,6 +306,11 @@
     for i in range(groups):
         g = turn(i, groups - 1)
         prepare_v(0, i)
+        if i == 0:
+            for entry in slots(1):
+                send_t(1, *entry)
+            send_round(2)
+            send_round(3)
         arrived(0, g + 1, 0)
         form_u(0, g + 1, group_rows(i))
         if i == 0:
@@ -316,11 +321,6 @@
             prepare_v(1, side)
         over_chunks(lambda c: first(c, i, side))
         if i == 0:
-            for entry in slots(1):
-                send_t(1, *entry)
-            send_round(2)
-            send_round(3)
-        if i == groups - 1:
             for r in range(4, rounds):
                 send_round(r)
     prepare_v(1, 2)

time: 47.4 us -> 47.5 us (level)
  no operation moved by 1% of the time
where the time goes in v5:
time: 47.5 us; the launch traced here: 47.3 us
  Pallas kernels  46 us (97%)
  local copies, waits for them, and re-layouts  1.32 us (3%)
    pallas_call x1, Pallas kernels, per_device(): pl.pallas_call(functools.partial(kernel, count, peers), out_shape=jax.Sha...  46 us
    unnamed x1, local copies, waits for them, and re-layouts  1.32 us

profile of v5, /device:TPU:25, one launch (start us, length us, event | category | flops | bytes accessed | tf_op | source)
XLA Modules:
  0.0 47.3 jit_solution(17311189966419200280)
XLA Ops:
  0.0 46.0 %back_transform.1 = f32[512,1024]{1,0:T(8,128)S(1)} custom-call(f32[512,1024]{1,0:T(8,128)} %eig.1, f32[6,64,512]{2,1,0:T(8,128)} %bitcast.1, f32[6,2,64,128]{3,2,1,0:T(8,128)} %fact.1), custom_call_target="tpu_custom_call" | custom-call | tf_op jit(solution)/shard_map/back_transform/pallas_call | solution.py:411
  46.0 1.3 %copy.5 = f32[512,1024]{1,0:T(8,128)} copy(f32[512,1024]{1,0:T(8,128)S(1)} %back_transform.1) | data formatting | bytes 4194304
